TPU v7x, 32 devices: a whole 2x2x4 slice. The times are simulated.
32 devices in a mesh: section: 8 (over y, x, core), slab: 4 (over z).
Axes of the slice: x: 2, y: 2, z: 4, core: 2. Of those that a mesh axis runs over, the one named last changes fastest.
Arguments:
- emitted: bfloat16 [8, 20, 512, 512], P('section', None, 'slab'), may hold values from -6 to 6
- returned: bfloat16 [8, 20, 512, 512], P('section', None, 'slab'), may hold values from -6 to 6
- stash: bfloat16 [8, 20, 512, 512], P('section', None, 'slab'), may hold values from -6 to 6
- skip_w: bfloat16 [8, 2, 20, 20], P('section'), may hold values from -1.25 to 1.25
- up_w: bfloat16 [8, 2, 80, 20], P('section'), may hold values from -1.25 to 1.25
- down_w: bfloat16 [8, 2, 20, 80], P('section'), may hold values from -0.625 to 0.625
- spec_w: bfloat16 [8, 2, 64, 2, 20, 20, 128], P('section', None, 'slab'), may hold values from -4 to 4
Outputs:
- sent: bfloat16 [8, 20, 512, 512], P('section', None, 'slab')
- back_grad: bfloat16 [8, 20, 512, 512], P('section', None, 'slab')
- grad_skip: float32 [8, 2, 20, 20], P('section')
- grad_up: float32 [8, 2, 80, 20], P('section')
- grad_down: float32 [8, 2, 20, 80], P('section')
- grad_spec: float32 [8, 2, 64, 2, 20, 20, 128], P('section', None, 'slab')
All inputs are finite; a program needn't handle non-finite values.
Results may differ from a plain program's by a relative error of at most 0.03.
Values may be sent and summed in bfloat16 or wider, within the bound.
A program may use at most 192 MiB of HBM per device.

v0:
```python
import jax
import jax.numpy as jnp
from jax import lax
from jax.sharding import PartitionSpec as P

M = 64
LAYERS = 2


root_two_pi = 0.7978845608028654
cubic_coef = 0.044715


def from_partner(array, axis, stride):
    return lax.ppermute(array, axis, [(i, i ^ 1 << stride) for i in range(lax.axis_size(axis))])


def passed_along(block, axis, distance):
    devices = range(lax.axis_size(axis))
    route = [((i - distance) % len(devices), i) for i in devices]
    return lax.ppermute(block, axis, route)


def smooth_gate(values):
    return (
        0.5
        * values
        * (1.0 + jnp.tanh(root_two_pi * (values + cubic_coef * values * values * values)))
    )


def gate_slope(values):
    tangent = jnp.tanh(root_two_pi * (values + cubic_coef * values * values * values))
    return 0.5 * (1.0 + tangent) + 0.5 * values * (1.0 - tangent * tangent) * root_two_pi * (
        1.0 + 3.0 * cubic_coef * values * values
    )


def angles(left_idx, right_idx, length):
    product_idx = left_idx[:, None] * right_idx[None, :] % length
    return 2.0 * jnp.pi / length * product_idx.astype(jnp.float32)


def tables(length, mode_count):
    cell_idx = jnp.arange(length, dtype=jnp.int32)
    low_modes = jnp.arange(mode_count, dtype=jnp.int32)
    both_modes = jnp.concatenate([low_modes, low_modes + (length - mode_count)])
    along_w = angles(cell_idx, low_modes, length)
    cos_w = jnp.cos(along_w)
    sin_w = jnp.sin(along_w)
    row_table = jnp.stack([cos_w, -sin_w], axis=1).astype(jnp.bfloat16)
    weight = jnp.where(low_modes == 0, 1.0, 2.0).astype(jnp.float32)[:, None]
    back_table = jnp.stack([weight * cos_w.T, -weight * sin_w.T], axis=1).astype(jnp.bfloat16)
    along_h = angles(cell_idx, both_modes, length)
    cos_h = jnp.cos(along_h)
    sin_h = jnp.sin(along_h)
    col_table = jnp.stack(
        [jnp.stack([cos_h, -sin_h], axis=1), jnp.stack([sin_h, cos_h], axis=1)], axis=0
    ).astype(jnp.bfloat16)
    return (row_table, back_table, col_table)


def product(form, left, right):
    return jnp.einsum(form, left, right, preferred_element_type=jnp.float32)


def to_modes(row_spec):
    return lax.all_to_all(row_spec, "slab", split_axis=0, concat_axis=3, tiled=True)


def to_rows(back_spec):
    return lax.all_to_all(back_spec, "slab", split_axis=3, concat_axis=0, tiled=True)


def fetch_saved(saved_input):
    top_bit = lax.axis_size("section").bit_length() - 1
    return from_partner(saved_input, "section", top_bit - 1)


def mix_modes(spec_layer, mode_spec):
    real_weight = spec_layer[:, 0]
    imag_weight = spec_layer[:, 1]
    real_mode = mode_spec[:, :, 0]
    imag_mode = mode_spec[:, :, 1]
    out_real = product("koix,kix->kox", real_weight, real_mode) - product(
        "koix,kix->kox", imag_weight, imag_mode
    )
    out_imag = product("koix,kix->kox", real_weight, imag_mode) + product(
        "koix,kix->kox", imag_weight, real_mode
    )
    return jnp.stack([out_real, out_imag], axis=1)


def mix_adjoint(spec_layer, mode_spec, grad_mixed):
    real_weight = spec_layer[:, 0]
    imag_weight = spec_layer[:, 1]
    real_mode = mode_spec[:, :, 0]
    imag_mode = mode_spec[:, :, 1]
    real_grad = grad_mixed[:, 0]
    imag_grad = grad_mixed[:, 1]
    grad_real = product("koix,kox->kix", real_weight, real_grad) + product(
        "koix,kox->kix", imag_weight, imag_grad
    )
    grad_imag = product("koix,kox->kix", real_weight, imag_grad) - product(
        "koix,kox->kix", imag_weight, real_grad
    )
    spec_real = product("kox,kix->koix", real_grad, real_mode) + product(
        "kox,kix->koix", imag_grad, imag_mode
    )
    spec_imag = product("kox,kix->koix", imag_grad, real_mode) - product(
        "kox,kix->koix", real_grad, imag_mode
    )
    return (jnp.stack([grad_real, grad_imag], axis=2), jnp.stack([spec_real, spec_imag], axis=1))


def layer_forward(activity, skip_layer, up_layer, down_layer, spec_layer, table_set):
    row_table, back_table, col_table = table_set
    length = activity.shape[2]
    row_spec = to_modes(product("chw,wpk->kpch", activity, row_table).astype(jnp.bfloat16))
    mode_spec = (product("kpch,phqx->kcqx", row_spec, col_table) / length).astype(jnp.bfloat16)
    mixed_modes = mix_modes(spec_layer, mode_spec).astype(jnp.bfloat16)
    back_spec = to_rows(product("kqcx,phqx->kpch", mixed_modes, col_table).astype(jnp.bfloat16))
    spectral = product("kpch,kpw->chw", back_spec, back_table) / length
    pre_act = spectral + product("oc,chw->ohw", skip_layer, activity)
    gated_act = smooth_gate(pre_act).astype(jnp.bfloat16)
    hidden = product("fc,chw->fhw", up_layer, gated_act)
    inner_act = smooth_gate(hidden).astype(jnp.bfloat16)
    result = (activity.astype(jnp.float32) + product("cf,fhw->chw", down_layer, inner_act)).astype(
        jnp.bfloat16
    )
    return (result, (activity, mode_spec, pre_act, gated_act, hidden, inner_act))


def layer_backward(grad_out, saved_act, skip_layer, up_layer, down_layer, spec_layer, table_set):
    row_table, back_table, col_table = table_set
    activity, mode_spec, pre_act, gated_act, hidden, inner_act = saved_act
    length = activity.shape[2]
    grad_inner = product("cf,chw->fhw", down_layer, grad_out)
    grad_down = product("chw,fhw->cf", grad_out, inner_act) / length
    grad_hidden = (grad_inner * gate_slope(hidden)).astype(jnp.bfloat16)
    grad_gated = product("fc,fhw->chw", up_layer, grad_hidden)
    grad_up = product("fhw,chw->fc", grad_hidden, gated_act) / length
    grad_pre = (grad_gated * gate_slope(pre_act)).astype(jnp.bfloat16)
    grad_skip = product("ohw,chw->oc", grad_pre, activity) / length
    grad_back = to_modes(
        (product("chw,kpw->kpch", grad_pre, back_table) / length).astype(jnp.bfloat16)
    )
    grad_mixed = product("kpch,phqx->kqcx", grad_back, col_table).astype(jnp.bfloat16)
    grad_modes, grad_spec = mix_adjoint(spec_layer, mode_spec, grad_mixed)
    grad_rows = to_rows(
        (product("kcqx,phqx->kpch", grad_modes.astype(jnp.bfloat16), col_table) / length).astype(
            jnp.bfloat16
        )
    )
    grad_field = (
        grad_out.astype(jnp.float32)
        + product("oc,ohw->chw", skip_layer, grad_pre)
        + product("kpch,wpk->chw", grad_rows, row_table)
    )
    return (grad_field.astype(jnp.bfloat16), grad_skip, grad_up, grad_down, grad_spec)


def shards(emitted, returned, stash, skip_w, up_w, down_w, spec_w):
    length = emitted.shape[3]
    table_set = tables(length, M)
    skip_section = skip_w[0]
    up_section = up_w[0]
    down_section = down_w[0]
    spec_section = spec_w[0]
    ahead_input = passed_along(emitted[0], "section", 1)
    top_grad = passed_along(returned[0], "section", -1)
    kept_input = fetch_saved(stash[0])
    activity = ahead_input
    for layer_idx in range(LAYERS):
        activity, unused_keep = layer_forward(
            activity,
            skip_section[layer_idx],
            up_section[layer_idx],
            down_section[layer_idx],
            spec_section[layer_idx],
            table_set,
        )
    sent_out = activity
    activity = kept_input
    saved_list = []
    for layer_idx in range(LAYERS):
        activity, layer_keep = layer_forward(
            activity,
            skip_section[layer_idx],
            up_section[layer_idx],
            down_section[layer_idx],
            spec_section[layer_idx],
            table_set,
        )
        saved_list.append(layer_keep)
    grad_now = top_grad
    skip_list, up_list, down_list, spec_list = ([], [], [], [])
    for layer_idx in reversed(range(LAYERS)):
        grad_now, grad_skip, grad_up, grad_down, grad_spec = layer_backward(
            grad_now,
            saved_list[layer_idx],
            skip_section[layer_idx],
            up_section[layer_idx],
            down_section[layer_idx],
            spec_section[layer_idx],
            table_set,
        )
        skip_list.insert(0, grad_skip)
        up_list.insert(0, grad_up)
        down_list.insert(0, grad_down)
        spec_list.insert(0, grad_spec)
    summed = lax.psum((jnp.stack(skip_list), jnp.stack(up_list), jnp.stack(down_list)), "slab")
    return (
        sent_out[None],
        grad_now[None],
        summed[0][None],
        summed[1][None],
        summed[2][None],
        jnp.stack(spec_list)[None],
    )


def solution(mesh):
    placed = (
        P("section", None, "slab", None),
        P("section", None, "slab", None),
        P("section", None, "slab", None),
        P("section", None, None, None),
        P("section", None, None, None),
        P("section", None, None, None),
        P("section", None, "slab", None, None, None, None),
    )
    return jax.shard_map(
        shards,
        mesh=mesh,
        in_specs=placed,
        out_specs=(
            P("section", None, "slab", None),
            P("section", None, "slab", None),
            P("section", None, None, None),
            P("section", None, None, None),
            P("section", None, None, None),
            P("section", None, "slab", None, None, None, None),
        ),
        check_vma=False,
    )
```

profile of v0, /device:TPU:0, one launch (start us, length us, event | category | flops | bytes accessed | tf_op | source)
XLA Modules:
  0.0 777.7 jit_solution(7025123289660281594)
XLA Ops:
  9.2 24.5 %collective-permute-done = bf16[20,128,512]{2,1,0:T(8,128)(2,1)S(1)} collective-permute-done((bf16[20,128,512]{2,1,0:T(8,128)(2,1)}, bf16[20,128,512]{2,1,0:T(8,128)(2,1)S(1)}, u32[]{:S(2)}, u32[]{:S(2)}) %collective-permute-start) | collective-permute-done | bytes 2621472 | tf_op jit(solution)/shard_map/ppermute | solution.py:21
  43.3 10.2 %fusion.372 = (bf16[1,1,16,2,20,20,128]{6,3,5,4,2,1,0:T(2,128)(2,1)}, bf16[1,1,16,2,20,20,128]{6,3,5,4,2,1,0:T(2,128)(2,1)}) fusion(bf16[1,2,16,2,20,20,128]{6,3,5,4,2,1,0:T(2,128)(2,1)} %param.13), kind=kLoop, calls=%fused_computation.447 | loop fusion | bytes 13107200 | tf_op jit(solution)/shard_map/slice | solution.py:180
  53.5 36.2 %collective-permute-done.2 = bf16[20,128,512]{2,1,0:T(8,128)(2,1)S(1)} collective-permute-done((bf16[20,128,512]{2,1,0:T(8,128)(2,1)}, bf16[20,128,512]{2,1,0:T(8,128)(2,1)S(1)}, u32[]{:S(2)}, u32[]{:S(2)}) %collective-permute-start.2) | collective-permute-done | bytes 2621472 | tf_op jit(solution)/shard_map/ppermute | solution.py:15
  136.6 10.4 %reshape.434 = bf16[4,2,40960]{2,1,0:T(2,128)(2,1)} reshape(bf16[512,2,16,20]{3,2,1,0:T(8,128)(2,1)} %bitcast.801) | data formatting | bytes 1310720
  160.5 10.1 %reshape.436 = bf16[4,2,40960]{2,1,0:T(2,128)(2,1)} reshape(bf16[512,2,16,20]{3,2,1,0:T(8,128)(2,1)} %bitcast.802) | data formatting | bytes 1310720
  188.0 11.3 %reshape.435 = bf16[512,2,16,20]{3,2,1,0:T(8,128)(2,1)} reshape(bf16[4,2,40960]{2,1,0:T(2,128)(2,1)S(1)} %all-to-all-done.1) | data formatting | bytes 1310720
  204.6 12.8 %reshape.437 = bf16[512,2,16,20]{3,2,1,0:T(8,128)(2,1)} reshape(bf16[4,2,40960]{2,1,0:T(2,128)(2,1)} %all-to-all-done.5) | data formatting | bytes 1310720
  229.9 13.2 %fusion.26 = f32[128,512,20]{1,2,0:T(8,128)} fusion(bf16[20,128,512]{2,1,0:T(8,128)(2,1)} %fusion.41, bf16[1,1,80,20]{2,1,3,0:T(2,128)(2,1)S(1)} %copy-done.65, bf16[1,1,20,80]{3,1,2,0:T(2,128)(2,1)S(1)} %copy-done.67), kind=kOutput, calls=%fused_computation.38 | convolution fusion | flops 466616320 | bytes 7870720 | tf_op jit(solution)/shard_map/cf,fhw->chw/dot_general | solution.py:64
  264.7 15.3 %multiply_convert_fusion.1 = (bf16[80,128,512]{2,0,1:T(8,128)(2,1)S(1)}, f32[128,512,80]{1,2,0:T(8,128)}) fusion(bf16[1,1,80,20]{2,1,3,0:T(2,128)(2,1)S(1)} %copy-done.65, bf16[20,128,512]{2,1,0:T(8,128)(2,1)S(1)} %get-tuple-element.110), kind=kOutput, calls=%fused_computation.35 | convolution fusion | flops 256901120 | bytes 34081920 | tf_op jit(solution)/shard_map/fc,chw->fhw/dot_general | solution.py:64
  331.8 10.1 %reshape.438 = bf16[4,2,40960]{2,1,0:T(2,128)(2,1)} reshape(bf16[512,2,16,20]{3,2,1,0:T(8,128)(2,1)} %bitcast.805) | data formatting | bytes 1310720
  357.7 10.1 %reshape.440 = bf16[4,2,40960]{2,1,0:T(2,128)(2,1)} reshape(bf16[512,2,16,20]{3,2,1,0:T(8,128)(2,1)} %bitcast.806) | data formatting | bytes 1310720
  385.8 11.7 %reshape.439 = bf16[512,2,16,20]{3,2,1,0:T(8,128)(2,1)} reshape(bf16[4,2,40960]{2,1,0:T(2,128)(2,1)S(1)} %all-to-all-done.3) | data formatting | bytes 1310720
  402.8 12.8 %reshape.441 = bf16[512,2,16,20]{3,2,1,0:T(8,128)(2,1)} reshape(bf16[4,2,40960]{2,1,0:T(2,128)(2,1)} %all-to-all-done.7) | data formatting | bytes 1310720
  441.6 13.4 %fusion.24 = f32[128,512,20]{1,2,0:T(8,128)} fusion(bf16[20,128,512]{2,1,0:T(8,128)(2,1)} %fusion.46, bf16[1,1,20,80]{3,1,2,0:T(2,128)(2,1)S(1)} %copy-done.72, bf16[1,1,80,20]{2,1,3,0:T(2,128)(2,1)S(1)} %copy-done.63), kind=kOutput, calls=%fused_computation.37 | convolution fusion | flops 466616320 | bytes 7870720 | tf_op jit(solution)/shard_map/cf,fhw->chw/dot_general | solution.py:64
  455.0 24.2 %fusion.18 = bf16[80,128,512]{2,0,1:T(8,128)(2,1)} fusion(f32[128,512,80]{1,2,0:T(8,128)} %fusion.109, bf16[20,128,512]{2,1,0:T(8,128)(2,1)} %collective-permute-done.1, bf16[1,1,20,80]{3,1,2,0:T(2,128)(2,1)S(1)} %copy-done.72), kind=kOutput, calls=%fused_computation.24 | convolution fusion | flops 309329920 | bytes 34081920 | tf_op jit(solution)/shard_map/cf,chw->fhw/dot_general | solution.py:64
  499.3 14.0 %fusion.252 = f32[1,20,80]{2,1,0:T(8,128)} fusion(bf16[20,128,512]{2,1,0:T(8,128)(2,1)} %collective-permute-done.1, f32[128,512,80]{1,2,0:T(8,128)} %fusion.109), kind=kOutput, calls=%fused_computation.257 | convolution fusion | flops 256902720 | bytes 23599360 | tf_op jit(solution)/shard_map/chw,fhw->cf/dot_general | solution.py:64
  542.9 10.0 %reshape.442 = bf16[4,2,40960]{2,1,0:T(2,128)(2,1)} reshape(bf16[512,2,16,20]{3,2,1,0:T(8,128)(2,1)} %bitcast.809) | data formatting | bytes 1310720
  575.4 11.3 %reshape.443 = bf16[512,2,16,20]{3,2,1,0:T(8,128)(2,1)} reshape(bf16[4,2,40960]{2,1,0:T(2,128)(2,1)S(1)} %all-to-all-done.9) | data formatting | bytes 1310720
  602.4 19.5 %fusion.23 = bf16[80,128,512]{2,0,1:T(8,128)(2,1)S(1)} fusion(f32[128,512,80]{1,2,0:T(8,128)} %get-tuple-element.113, bf16[20,128,512]{2,0,1:T(8,128)(2,1)S(1)} %fusion.36, bf16[1,1,20,80]{3,1,2,0:T(2,128)(2,1)S(1)} %copy-done.69), kind=kOutput, calls=%fused_computation.29 | convolution fusion | flops 309329920 | bytes 34081920 | tf_op jit(solution)/shard_map/cf,chw->fhw/dot_general | solution.py:64
  656.8 20.9 %all-reduce = (f32[1,2,20,20]{3,2,1,0:T(8,128)S(1)}, f32[1,2,80,20]{2,3,1,0:T(8,128)S(1)}, f32[1,2,20,80]{3,2,1,0:T(8,128)S(1)}) all-reduce(f32[1,2,20,20]{3,2,1,0:T(8,128)S(1)} %maximum_bitcast_fusion.17, f32[1,2,80,20]{2,3,1,0:T(8,128)S(1)} %maximum_bitcast_fusion.18, ...), channel_id=1, replica_groups=mesh['section'=8,'slab'=4] {'slab'}, use_global_device_ids=true, to_apply=%region_0.1 | all-reduce | flops 7200 | bytes 57600 | tf_op jit(solution)/shard_map/psum | solution.py:212
  697.0 10.1 %reshape.444 = bf16[4,2,40960]{2,1,0:T(2,128)(2,1)} reshape(bf16[512,2,16,20]{3,2,1,0:T(8,128)(2,1)} %bitcast.811) | data formatting | bytes 1310720
  714.8 11.1 %maximum_bitcast_fusion = f32[1,2,16,2,20,20,128]{6,2,5,4,3,1,0:T(8,128)} fusion(f32[1,16,2,20,20,128]{5,1,4,3,2,0:T(8,128)} %maximum_bitcast_fusion.2, f32[1,16,2,20,20,128]{5,1,4,3,2,0:T(8,128)} %maximum_bitcast_fusion.1), kind=kLoop, calls=%fused_computation.36 | loop fusion | flops 3276800 | bytes 26214400 | tf_op jit(solution)/shard_map/broadcast_in_dim | solution.py:219
  726.0 23.9 %copy.347 = f32[1,2,16,2,20,20,128]{6,3,5,4,2,1,0:T(2,128)} copy(f32[1,2,16,2,20,20,128]{6,2,5,4,3,1,0:T(8,128)} %maximum_bitcast_fusion) | data formatting | bytes 26214400
  749.9 11.3 %reshape.445 = bf16[512,2,16,20]{3,2,1,0:T(8,128)(2,1)} reshape(bf16[4,2,40960]{2,1,0:T(2,128)(2,1)S(1)} %all-to-all-done.11) | data formatting | bytes 1310720
  (342 shorter events, 416.5 us)
Async XLA Ops:
  0.6 33.1 %collective-permute-start = (bf16[20,128,512]{2,1,0:T(8,128)(2,1)}, bf16[20,128,512]{2,1,0:T(8,128)(2,1)S(1)}, u32[]{:S(2)}, u32[]{:S(2)}) collective-permute-start(bf16[20,128,512]{2,1,0:T(8,128)(2,1)} %bitcast.843), channel_id=1, source_target_pairs={{28,0},{0,4},{4,8},{8,12},{12,16},{16,20},{20,24},{24,28},{29,1},{... | collective-permute-start | bytes 7864328 | tf_op jit(solution)/shard_map/ppermute | solution.py:21
  1.2 88.5 %collective-permute-start.2 = (bf16[20,128,512]{2,1,0:T(8,128)(2,1)}, bf16[20,128,512]{2,1,0:T(8,128)(2,1)S(1)}, u32[]{:S(2)}, u32[]{:S(2)}) collective-permute-start(bf16[20,128,512]{2,1,0:T(8,128)(2,1)} %bitcast.844), channel_id=1, source_target_pairs={{0,16},{4,20},{8,24},{12,28},{16,0},{20,4},{24,8},{28,12},{1,17},{... | collective-permute-start | bytes 7864328 | tf_op jit(solution)/shard_map/ppermute | solution.py:15
  4.4 283.4 %copy-start.25 = (bf16[512,1,64]{0,2,1:T(8,128)(2,1)}, bf16[512,1,64]{0,2,1:T(8,128)(2,1)S(1)}, u32[]{:S(2)}) copy-start(bf16[512,1,64]{0,2,1:T(8,128)(2,1)S(1)} %get-tuple-element.116) | copy-start | bytes 196612
  4.4 283.4 %copy-start.27 = (bf16[512,1,64]{0,2,1:T(8,128)(2,1)}, bf16[512,1,64]{0,2,1:T(8,128)(2,1)S(1)}, u32[]{:S(2)}) copy-start(bf16[512,1,64]{0,2,1:T(8,128)(2,1)S(1)} %get-tuple-element.117) | copy-start | bytes 196612
  7.8 174.8 %copy-start.60 = (bf16[1,1,20,20]{3,1,2,0:T(2,128)(2,1)}, bf16[1,1,20,20]{3,1,2,0:T(2,128)(2,1)S(1)}, u32[]{:S(2)}) copy-start(bf16[1,1,20,20]{3,1,2,0:T(2,128)(2,1)S(1)} %get-tuple-element.106) | copy-start | bytes 2404
  37.7 54.5 %all-to-all-start = ((bf16[64,2,20,128]{3,1,2,0:T(2,128)(2,1)}), bf16[64,2,20,128]{3,1,2,0:T(2,128)(2,1)S(1)}, u32[]{:S(2)}, u32[]{:S(2)}) async-start(bf16[64,2,20,128]{3,1,2,0:T(2,128)(2,1)} %copy.253), calls=%async_computation | async-start | bytes 1310720 | tf_op jit(solution)/shard_map/all_to_all | solution.py:68
  92.2 23.1 %all-to-all-start.4 = ((bf16[64,2,20,128]{3,1,2,0:T(2,128)(2,1)}), bf16[64,2,20,128]{3,1,2,0:T(2,128)(2,1)}, u32[]{:S(2)}, u32[]{:S(2)}) async-start(bf16[64,2,20,128]{3,1,2,0:T(2,128)(2,1)} %copy.285), calls=%async_computation.4 | async-start | bytes 1310720 | tf_op jit(solution)/shard_map/all_to_all | solution.py:68
  147.0 23.5 %all-to-all-start.1 = ((bf16[4,2,40960]{2,1,0:T(2,128)(2,1)}), bf16[4,2,40960]{2,1,0:T(2,128)(2,1)S(1)}, u32[]{:S(2)}, u32[]{:S(2)}) async-start(bf16[4,2,40960]{2,1,0:T(2,128)(2,1)} %reshape.434), calls=%async_computation.1 | async-start | bytes 1310720 | tf_op jit(solution)/shard_map/all_to_all | solution.py:72
  151.1 106.6 %copy-start.47 = (bf16[64,1,512]{2,0,1:T(8,128)(2,1)}, bf16[64,1,512]{2,0,1:T(8,128)(2,1)S(1)}, u32[]{:S(2)}) copy-start(bf16[64,1,512]{2,0,1:T(8,128)(2,1)S(1)} %get-tuple-element.121) | copy-start | bytes 196612
  170.5 34.1 %all-to-all-start.5 = ((bf16[4,2,40960]{2,1,0:T(2,128)(2,1)}), bf16[4,2,40960]{2,1,0:T(2,128)(2,1)}, u32[]{:S(2)}, u32[]{:S(2)}) async-start(bf16[4,2,40960]{2,1,0:T(2,128)(2,1)} %reshape.436), calls=%async_computation.5 | async-start | bytes 1310720 | tf_op jit(solution)/shard_map/all_to_all | solution.py:72
  249.6 125.7 %copy-start.1 = (bf16[20,128,512]{2,1,0:T(8,128)(2,1)}, bf16[20,128,512]{2,1,0:T(8,128)(2,1)S(1)}, u32[]{:S(2)}) copy-start(bf16[20,128,512]{2,1,0:T(8,128)(2,1)S(1)} %fusion.64) | copy-start | bytes 7864324
  252.1 39.6 %all-to-all-start.2 = ((bf16[64,2,20,128]{3,1,2,0:T(2,128)(2,1)}), bf16[64,2,20,128]{3,1,2,0:T(2,128)(2,1)S(1)}, u32[]{:S(2)}, u32[]{:S(2)}) async-start(bf16[64,2,20,128]{3,1,2,0:T(2,128)(2,1)} %copy.268), calls=%async_computation.2 | async-start | bytes 1310720 | tf_op jit(solution)/shard_map/all_to_all | solution.py:68
  291.8 20.6 %all-to-all-start.6 = ((bf16[64,2,20,128]{3,1,2,0:T(2,128)(2,1)}), bf16[64,2,20,128]{3,1,2,0:T(2,128)(2,1)}, u32[]{:S(2)}, u32[]{:S(2)}) async-start(bf16[64,2,20,128]{3,1,2,0:T(2,128)(2,1)} %copy.296), calls=%async_computation.6 | async-start | bytes 1310720 | tf_op jit(solution)/shard_map/all_to_all | solution.py:68
  341.9 25.9 %all-to-all-start.3 = ((bf16[4,2,40960]{2,1,0:T(2,128)(2,1)}), bf16[4,2,40960]{2,1,0:T(2,128)(2,1)S(1)}, u32[]{:S(2)}, u32[]{:S(2)}) async-start(bf16[4,2,40960]{2,1,0:T(2,128)(2,1)} %reshape.438), calls=%async_computation.3 | async-start | bytes 1310720 | tf_op jit(solution)/shard_map/all_to_all | solution.py:72
  367.8 35.0 %all-to-all-start.7 = ((bf16[4,2,40960]{2,1,0:T(2,128)(2,1)}), bf16[4,2,40960]{2,1,0:T(2,128)(2,1)}, u32[]{:S(2)}, u32[]{:S(2)}) async-start(bf16[4,2,40960]{2,1,0:T(2,128)(2,1)} %reshape.440), calls=%async_computation.7 | async-start | bytes 1310720 | tf_op jit(solution)/shard_map/all_to_all | solution.py:72
  372.8 82.2 %collective-permute-start.1 = (bf16[20,128,512]{2,1,0:T(8,128)(2,1)}, bf16[20,128,512]{2,1,0:T(8,128)(2,1)}, u32[]{:S(2)}, u32[]{:S(2)}) collective-permute-start(bf16[20,128,512]{2,1,0:T(8,128)(2,1)} %bitcast.845), channel_id=1, source_target_pairs={{4,0},{8,4},{12,8},{16,12},{20,16},{24,20},{28,24},{0,28},{5,1},{9... | collective-permute-start | bytes 7864328 | tf_op jit(solution)/shard_map/ppermute | solution.py:21
  441.6 42.6 %slice-start.7 = ((s8[5242880]{0:T(1024)(128)(4,1)}), s8[1048576]{0:T(1024)(128)(4,1)S(1)}, s32[]{:S(2)}) async-start(s8[5242880]{0:T(1024)(128)(4,1)} %bitcast.817), calls=%async_computation.19 | async-start | bytes 2097152
  455.0 29.2 %slice-start.8 = ((s8[5242880]{0:T(1024)(128)(4,1)}), s8[4194304]{0:T(1024)(128)(4,1)S(1)}, s32[]{:S(2)}) async-start(s8[5242880]{0:T(1024)(128)(4,1)} %bitcast.817), calls=%async_computation.20 | async-start | bytes 8388608
  494.0 31.9 %all-to-all-start.8 = ((bf16[64,2,20,128]{3,1,2,0:T(2,128)(2,1)}), bf16[64,2,20,128]{3,1,2,0:T(2,128)(2,1)}, u32[]{:S(2)}, u32[]{:S(2)}) async-start(bf16[64,2,20,128]{3,1,2,0:T(2,128)(2,1)} %copy.309), calls=%async_computation.8 | async-start | bytes 1310720 | tf_op jit(solution)/shard_map/all_to_all | solution.py:68
  552.9 22.5 %all-to-all-start.9 = ((bf16[4,2,40960]{2,1,0:T(2,128)(2,1)}), bf16[4,2,40960]{2,1,0:T(2,128)(2,1)S(1)}, u32[]{:S(2)}, u32[]{:S(2)}) async-start(bf16[4,2,40960]{2,1,0:T(2,128)(2,1)} %reshape.442), calls=%async_computation.9 | async-start | bytes 1310720 | tf_op jit(solution)/shard_map/all_to_all | solution.py:72
  602.4 48.9 %copy-start.7 = (bf16[20,128,512]{2,0,1:T(8,128)(2,1)}, bf16[20,128,512]{2,0,1:T(8,128)(2,1)S(1)}, u32[]{:S(2)}) copy-start(bf16[20,128,512]{2,0,1:T(8,128)(2,1)S(1)} %fusion.36) | copy-start | bytes 7864324
  638.1 41.5 %all-to-all-start.10 = ((bf16[64,2,20,128]{3,1,2,0:T(2,128)(2,1)}), bf16[64,2,20,128]{3,1,2,0:T(2,128)(2,1)}, u32[]{:S(2)}, u32[]{:S(2)}) async-start(bf16[64,2,20,128]{3,1,2,0:T(2,128)(2,1)} %copy.320), calls=%async_computation.10 | async-start | bytes 1310720 | tf_op jit(solution)/shard_map/all_to_all | solution.py:68
  656.8 31.0 %copy-start.4 = (bf16[16,2,20,20,128]{4,0,3,2,1:T(8,128)(2,1)S(1)}, bf16[16,2,20,20,128]{4,0,3,2,1:T(8,128)(2,1)}, u32[]{:S(2)}) copy-start(bf16[16,2,20,20,128]{4,0,3,2,1:T(8,128)(2,1)} %copy-done.3) | copy-start | bytes 9830404
  707.1 42.8 %all-to-all-start.11 = ((bf16[4,2,40960]{2,1,0:T(2,128)(2,1)}), bf16[4,2,40960]{2,1,0:T(2,128)(2,1)S(1)}, u32[]{:S(2)}, u32[]{:S(2)}) async-start(bf16[4,2,40960]{2,1,0:T(2,128)(2,1)} %reshape.444), calls=%async_computation.11 | async-start | bytes 1310720 | tf_op jit(solution)/shard_map/all_to_all | solution.py:72
  (73 other events, 844.4 us)
where the time goes:
time: 786 us; the launch traced here: 778 us
  local copies, waits for them, and re-layouts  311 us (40%)
  matrix products  231 us (29%)
  waiting for transfers between devices  78.2 us (10%)
  other arithmetic  72.4 us (9%)
  starting transfers between devices  60.9 us (8%)
  blocking collectives  20.9 us (3%)
    dot_general x45, matrix products, product(): return jnp.einsum(form, left, right, preferred_element_type=jnp.float32)  231 us
    unnamed x193, local copies, waits for them, and re-layouts  171 us
    ppermute x1, waiting for transfers between devices, from_partner(): lax.ppermute(array, axis, [(i, i ^ 1 << stride) for i in range(lax.axis_s...  36.2 us
    all_to_all x12, local copies, waits for them, and re-layouts, to_rows(): lax.all_to_all(back_spec, 'slab', split_axis=3, concat_axis=0, tiled=True)  34.7 us
    all_to_all x6, starting transfers between devices, to_modes(): lax.all_to_all(row_spec, 'slab', split_axis=0, concat_axis=3, tiled=True)  31.3 us
    convert_element_type x4, local copies, waits for them, and re-layouts, layer_forward(): product('kqcx,phqx->kpch', mixed_modes, col_table).astype(jnp.bfloat16)  30.3 us
    all_to_all x6, starting transfers between devices, to_rows(): lax.all_to_all(back_spec, 'slab', split_axis=3, concat_axis=0, tiled=True)  26.4 us
    ppermute x2, waiting for transfers between devices, passed_along(): return lax.ppermute(block, axis, route)  24.5 us
  transfers between devices with their start and end apart: 15, of which 5 were waited for; matrix products, arithmetic and copies ran while one was open for 40% of the time, Pallas kernels for 0%

commit v1 on v0

--- a/solution.py
+++ b/solution.py
@@ -1,6 +1,9 @@
 import jax
 import jax.numpy as jnp
+import numpy as np
 from jax import lax
+from jax.experimental import pallas as pl
+from jax.experimental.pallas import tpu as pltpu
 from jax.sharding import PartitionSpec as P
 
 M = 64
@@ -220,6 +223,437 @@
     )
 
 
+BF = jnp.bfloat16
+F32 = jnp.float32
+VM = 60 * 1024 * 1024
+
+
+def fast_tables(length, mode_count, groups):
+    ang = lambda a, b: (np.float32(2.0 * np.pi / length) * ((a[:, None] * b[None, :]) % length).astype(np.float32))
+    cells = np.arange(length)
+    low = np.arange(mode_count)
+    both = np.concatenate([low, low + (length - mode_count)])
+    along = ang(low, cells)
+    cos_w, sin_w = np.cos(along), np.sin(along)
+    weight = np.where(low == 0, 1.0, 2.0).astype(np.float32)[:, None]
+
+    def grouped(a, b):
+        a = a.reshape(groups, 1, mode_count // groups, length)
+        b = b.reshape(groups, 1, mode_count // groups, length)
+        return np.concatenate([a, b], axis=1).reshape(2 * mode_count, length)
+
+    row = grouped(cos_w, -sin_w)
+    back = grouped(weight * cos_w, -weight * sin_w)
+    along_h = ang(cells, both)
+    cos_h, sin_h = np.cos(along_h), np.sin(along_h)
+    col = np.stack([np.concatenate([cos_h, -sin_h], 1), np.concatenate([sin_h, cos_h], 1)], 0)
+    modes = col.shape[2]
+    col = col.reshape(2, groups, length // groups, modes).transpose(1, 0, 2, 3).reshape(2 * length, modes)
+    made = lambda t: jnp.asarray(t.astype(BF))
+    return made(row), made(row.T), made(back), made(back.T), made(col), made(col.T)
+
+
+def call(body, grid, ins, outs, scratch, aliases=None, cost=(0, 0)):
+    return pl.pallas_call(
+        body,
+        grid=grid,
+        in_specs=ins,
+        out_specs=outs[0],
+        out_shape=outs[1],
+        scratch_shapes=scratch,
+        input_output_aliases=aliases or {},
+        compiler_params=pltpu.CompilerParams(
+            dimension_semantics=("arbitrary",) * len(grid), vmem_limit_bytes=VM
+        ),
+        cost_estimate=pl.CostEstimate(flops=cost[0], bytes_accessed=cost[1], transcendentals=0),
+    )
+
+
+def same(shape):
+    return pl.BlockSpec(shape, lambda i: (0,) * len(shape))
+
+
+def dot(a, b, ca=1, cb=0):
+    return lax.dot_general(a, b, (((ca,), (cb,)), ((), ())), preferred_element_type=F32)
+
+
+def first_rows(field, row):
+    C, H, W = field.shape
+    J = row.shape[0]
+    cb = next(n for n in (5, 4, 2, 1) if C % n == 0)
+
+    def body(v_ref, row_ref, out_ref):
+        v = v_ref[...].reshape(cb * H, W)
+        out_ref[...] = dot(row_ref[...], v, 1, 1).astype(BF)
+
+    return call(
+        body, (C // cb,),
+        [pl.BlockSpec((cb, H, W), lambda i: (i, 0, 0)), same((J, W))],
+        (pl.BlockSpec((J, cb * H), lambda i: (0, i)), jax.ShapeDtypeStruct((J, C * H), BF)),
+        [], cost=(2 * J * C * H * W, 2 * C * H * W),
+    )(field, row)
+
+
+def gather_modes(src_ref, lhs, C, S, K, H):
+    for c in range(C):
+        for s in range(S):
+            for p in range(2):
+                j = s * 2 + p
+                lhs[c * K:(c + 1) * K, j * H:(j + 1) * H] = src_ref[s, p * K:(p + 1) * K, c * H:(c + 1) * H]
+
+
+def spread_modes(wide, out_ref, C, S, K, H):
+    for c in range(C):
+        for s in range(S):
+            for p in range(2):
+                j = s * 2 + p
+                out_ref[s, p * K:(p + 1) * K, c * H:(c + 1) * H] = wide[c * K:(c + 1) * K, j * H:(j + 1) * H].astype(BF)
+
+
+def split_parts(wide, parts):
+    rows, X = parts.shape
+    parts[:rows // 2, :] = wide[:, :X]
+    parts[rows // 2:, :] = wide[:, X:]
+
+
+def joined_parts(parts):
+    rows = parts.shape[0] // 2
+    return jnp.concatenate([parts[:rows, :], parts[rows:, :]], axis=1).astype(BF)
+
+
+def modes_forward(spec, layer, src, col, col_t, length):
+    _, K, _, C, _, X = spec.shape
+    S, _, CH = src.shape
+    H = CH // C
+
+    def body(r_ref, src_ref, col_ref, colt_ref, out_ref, x_ref, lhs, xs, ys):
+        k = pl.program_id(0)
+
+        @pl.when(k == 0)
+        def _():
+            gather_modes(src_ref, lhs, C, S, K, H)
+            x_ref[...] = (dot(lhs[...], col_ref[...]) / length).astype(BF)
+            split_parts(x_ref[...].astype(F32), xs)
+
+        real, imag = pl.ds(k, C, stride=K), pl.ds(C * K + k, C, stride=K)
+        xr = xs[real, :][None]
+        xi = xs[imag, :][None]
+        rr = r_ref[0, 0, 0].astype(F32)
+        ri = r_ref[0, 0, 1].astype(F32)
+        ys[real, :] = jnp.sum(rr * xr - ri * xi, axis=1)
+        ys[imag, :] = jnp.sum(rr * xi + ri * xr, axis=1)
+
+        @pl.when(k == K - 1)
+        def _():
+            spread_modes(dot(joined_parts(ys), colt_ref[...]), out_ref, C, S, K, H)
+
+    J = col.shape[0]
+    return call(
+        body, (K,),
+        [pl.BlockSpec((1, 1, 2, C, C, X), lambda i: (layer, i, 0, 0, 0, 0)), same(src.shape), same(col.shape), same(col_t.shape)],
+        ([same(src.shape), same((C * K, 2 * X))],
+         [jax.ShapeDtypeStruct(src.shape, BF), jax.ShapeDtypeStruct((C * K, 2 * X), BF)]),
+        [pltpu.VMEM((C * K, J), BF), pltpu.VMEM((2 * C * K, X), F32), pltpu.VMEM((2 * C * K, X), F32)],
+        cost=(8 * C * K * J * X, 8 * K * C * C * X),
+    )(spec, src, col, col_t)
+
+
+def modes_backward(spec, layer, src, kept_modes, col, col_t, length, held):
+    L, K, _, C, _, X = spec.shape
+    S, _, CH = src.shape
+    H = CH // C
+
+    def body(r_ref, src_ref, m_ref, col_ref, colt_ref, *rest):
+        out_ref, grad_ref, lhs, xs, gs, ys = rest[-6:]
+        k = pl.program_id(0)
+
+        @pl.when(k == 0)
+        def _():
+            gather_modes(src_ref, lhs, C, S, K, H)
+            split_parts(dot(lhs[...], col_ref[...]).astype(BF).astype(F32), gs)
+            split_parts(m_ref[...].astype(F32), xs)
+
+        real, imag = pl.ds(k, C, stride=K), pl.ds(C * K + k, C, stride=K)
+        xr = xs[real, :][None]
+        xi = xs[imag, :][None]
+        gr = gs[real, :][:, None, :]
+        gi = gs[imag, :][:, None, :]
+        rr = r_ref[0, 0, 0].astype(F32)
+        ri = r_ref[0, 0, 1].astype(F32)
+        ys[real, :] = jnp.sum(rr * gr + ri * gi, axis=0)
+        ys[imag, :] = jnp.sum(rr * gi - ri * gr, axis=0)
+        grad_ref[0, 0, 0] = gr * xr + gi * xi
+        grad_ref[0, 0, 1] = gi * xr - gr * xi
+
+        @pl.when(k == K - 1)
+        def _():
+            spread_modes(dot(joined_parts(ys), colt_ref[...]) / length, out_ref, C, S, K, H)
+
+    J = col.shape[0]
+    block = pl.BlockSpec((1, 1, 2, C, C, X), lambda i: (layer, i, 0, 0, 0, 0))
+    ins = [block, same(src.shape), same(kept_modes.shape), same(col.shape), same(col_t.shape)]
+    args = [spec, src, kept_modes, col, col_t]
+    aliases = {}
+    if held is not None:
+        ins.append(pl.BlockSpec(memory_space=pl.ANY))
+        args.append(held)
+        aliases = {5: 1}
+    return call(
+        body, (K,), ins,
+        ([same(src.shape), block], [jax.ShapeDtypeStruct(src.shape, BF), jax.ShapeDtypeStruct(spec.shape, F32)]),
+        [pltpu.VMEM((C * K, J), BF)] + [pltpu.VMEM((2 * C * K, X), F32)] * 3,
+        aliases, cost=(8 * C * K * J * X, 16 * K * C * C * X),
+    )(*args)
+
+
+def load_rows(src_ref, turned, C, CP, H):
+    J = turned.shape[1]
+    turned[...] = jnp.zeros_like(turned)
+    for c in range(C):
+        tile = src_ref[:, c * H:(c + 1) * H].astype(F32)
+        turned[pl.ds(c, H, stride=CP), :] = tile.T
+
+
+def store_rows(turned, out_ref, C, CP, H):
+    for c in range(C):
+        tile = turned[pl.ds(c, H, stride=CP), :]
+        out_ref[:, c * H:(c + 1) * H] = tile.T.astype(BF)
+
+
+def tanh_of(t, t2):
+    return jnp.tanh(t * (root_two_pi + (root_two_pi * cubic_coef) * t2))
+
+
+def gate(t):
+    half = 0.5 * t
+    return half + half * tanh_of(t, t * t)
+
+
+def gate_pair(t):
+    t2 = t * t
+    th = tanh_of(t, t2)
+    near = 0.5 + 0.5 * th
+    half = 0.5 * t
+    slope = near + half * (1.0 - th * th) * (root_two_pi + (3.0 * cubic_coef * root_two_pi) * t2)
+    return t * near, slope
+
+
+HB = 16
+
+
+def field_forward(v, src, skip, up, down, back, row_t, length, want_rows):
+    H, CP, W = v.shape
+    J = back.shape[0]
+    C = src.shape[1] // H
+    F = up.shape[0]
+    steps = H // HB
+
+    def body(v_ref, src_ref, skip_ref, up_ref, down_ref, back_ref, rowt_ref, *rest):
+        if want_rows:
+            out_ref, rows_ref, turned, zs, made = rest
+        else:
+            out_ref, turned, zs = rest
+        i = pl.program_id(0)
+
+        @pl.when(i == 0)
+        def _():
+            load_rows(src_ref, turned, C, CP, H)
+
+        at = pl.ds(pl.multiple_of(i * HB * CP, HB * CP), HB * CP)
+        zs[...] = dot(turned[at, :].astype(BF), back_ref[...]) / length
+
+        def one(h, carry):
+            vh = v_ref[h]
+            z = zs[pl.ds(pl.multiple_of(h * CP, CP), CP), :] + dot(skip_ref[...], vh)
+            y = gate(z).astype(BF)
+            act = gate(dot(up_ref[...], y)).astype(BF)
+            out_ref[h] = (vh.astype(F32) + dot(down_ref[...], act)).astype(BF)
+            return carry
+
+        lax.fori_loop(0, HB, one, 0, unroll=4)
+        if want_rows:
+            made[at, :] = dot(out_ref[...].reshape(HB * CP, W), rowt_ref[...])
+
+            @pl.when(i == steps - 1)
+            def _():
+                store_rows(made, rows_ref, C, CP, H)
+
+    block = pl.BlockSpec((HB, CP, W), lambda i: (i, 0, 0))
+    outs = ([block], [jax.ShapeDtypeStruct(v.shape, BF)])
+    scratch = [pltpu.VMEM((H * CP, J), F32), pltpu.VMEM((HB * CP, W), F32)]
+    if want_rows:
+        outs[0].append(same((J, C * H)))
+        outs[1].append(jax.ShapeDtypeStruct((J, C * H), BF))
+        scratch.append(pltpu.VMEM((H * CP, J), F32))
+    return call(
+        body, (steps,),
+        [block, same(src.shape), same(skip.shape), same(up.shape), same(down.shape), same(back.shape), same(row_t.shape)],
+        outs, scratch, cost=(4 * H * CP * W * (F + J), 4 * H * CP * W),
+    )(v, src, skip, up, down, back, row_t)
+
+
+def field_backward(v, g, src, skip, up, down, up_t, down_t, back, back_t, length):
+    H, CP, W = v.shape
+    J = back.shape[0]
+    C = src.shape[1] // H
+    F = up.shape[0]
+    steps = H // HB
+
+    def body(v_ref, g_ref, src_ref, skip_ref, up_ref, down_ref, upt_ref, downt_ref, back_ref, backt_ref,
+             gz_ref, rows_ref, gskip_ref, gup_ref, gdown_ref, turned, zs, made):
+        i = pl.program_id(0)
+
+        @pl.when(i == 0)
+        def _():
+            load_rows(src_ref, turned, C, CP, H)
+            gskip_ref[...] = jnp.zeros_like(gskip_ref)
+            gup_ref[...] = jnp.zeros_like(gup_ref)
+            gdown_ref[...] = jnp.zeros_like(gdown_ref)
+
+        at = pl.ds(pl.multiple_of(i * HB * CP, HB * CP), HB * CP)
+        zs[...] = dot(turned[at, :].astype(BF), back_ref[...]) / length
+
+        def one(h, carry):
+            vh = v_ref[h]
+            gh = g_ref[h]
+            z = zs[pl.ds(pl.multiple_of(h * CP, CP), CP), :] + dot(skip_ref[...], vh)
+            y, y_slope = gate_pair(z)
+            y = y.astype(BF)
+            act, act_slope = gate_pair(dot(up_ref[...], y))
+            act = act.astype(BF)
+            grad_hidden = (dot(downt_ref[...], gh) * act_slope).astype(BF)
+            gz = (dot(upt_ref[...], grad_hidden) * y_slope).astype(BF)
+            gz_ref[h] = gz
+            gdown_ref[...] += dot(gh, act, 1, 1)
+            gup_ref[...] += dot(grad_hidden, y, 1, 1)
+            gskip_ref[...] += dot(gz, vh, 1, 1)
+            return carry
+
+        lax.fori_loop(0, HB, one, 0, unroll=2)
+        made[at, :] = dot(gz_ref[...].reshape(HB * CP, W), backt_ref[...]) / length
+
+        @pl.when(i == steps - 1)
+        def _():
+            store_rows(made, rows_ref, C, CP, H)
+
+    block = pl.BlockSpec((HB, CP, W), lambda i: (i, 0, 0))
+    args = (v, g, src, skip, up, down, up_t, down_t, back, back_t)
+    small = [(CP, CP), (F, CP), (CP, F)]
+    return call(
+        body, (steps,),
+        [block, block] + [same(a.shape) for a in args[2:]],
+        ([block, same((J, C * H))] + [same(s) for s in small],
+         [jax.ShapeDtypeStruct(v.shape, BF), jax.ShapeDtypeStruct((J, C * H), BF)]
+         + [jax.ShapeDtypeStruct(s, F32) for s in small]),
+        [pltpu.VMEM((H * CP, J), F32), pltpu.VMEM((HB * CP, W), F32), pltpu.VMEM((H * CP, J), F32)],
+        cost=(8 * H * CP * W * (F + J), 6 * H * CP * W),
+    )(*args)
+
+
+def field_grad(g, gz, src, skip_t, row):
+    H, CP, W = g.shape
+    J = row.shape[0]
+    C = src.shape[1] // H
+    steps = H // HB
+
+    def body(g_ref, gz_ref, src_ref, skipt_ref, row_ref, out_ref, turned, zs):
+        i = pl.program_id(0)
+
+        @pl.when(i == 0)
+        def _():
+            load_rows(src_ref, turned, C, CP, H)
+
+        at = pl.ds(pl.multiple_of(i * HB * CP, HB * CP), HB * CP)
+        zs[...] = dot(turned[at, :].astype(BF), row_ref[...])
+
+        def one(h, carry):
+            here = pl.ds(pl.multiple_of(h * CP, CP), CP)
+            out_ref[h] = (g_ref[h].astype(F32) + dot(skipt_ref[...], gz_ref[h]) + zs[here, :]).astype(BF)
+            return carry
+
+        lax.fori_loop(0, HB, one, 0, unroll=4)
+
+    block = pl.BlockSpec((HB, CP, W), lambda i: (i, 0, 0))
+    return call(
+        body, (steps,),
+        [block, block, same(src.shape), same(skip_t.shape), same(row.shape)],
+        (block, jax.ShapeDtypeStruct(g.shape, BF)),
+        [pltpu.VMEM((H * CP, J), F32), pltpu.VMEM((HB * CP, W), F32)],
+        cost=(2 * H * CP * W * J, 6 * H * CP * W),
+    )(g, gz, src, skip_t, row)
+
+
+def exchanged(spectra, groups):
+    blocks = spectra.reshape(groups, spectra.size // spectra.shape[-1] // groups, spectra.shape[-1])
+    return lax.all_to_all(blocks, "slab", split_axis=0, concat_axis=0, tiled=True)
+
+
+def fast_shards(emitted, returned, stash, skip_w, up_w, down_w, spec_w):
+    _, C, H, W = emitted.shape
+    L = spec_w.shape[1]
+    S = lax.axis_size("slab")
+    mode_count = spec_w.shape[2] * S
+    CP = -(-C // 16) * 16
+    row, row_t, back, back_t, col, col_t = fast_tables(W, mode_count, S)
+    spec = spec_w[0]
+    pad = CP - C
+    skip = jnp.pad(skip_w[0], ((0, 0), (0, pad), (0, pad)))
+    up = jnp.pad(up_w[0], ((0, 0), (0, 0), (0, pad)))
+    down = jnp.pad(down_w[0], ((0, 0), (0, pad), (0, 0)))
+    turn = lambda a: jnp.swapaxes(a, 1, 2)
+    skip_t, up_t, down_t = turn(skip), turn(up), turn(down)
+    size = lax.axis_size("section")
+    lined = lambda f: jnp.pad(jnp.swapaxes(f, 0, 1), ((0, 0), (0, pad), (0, 0)))
+    plain = lambda f: jnp.swapaxes(f[:, :C], 0, 1)
+    flat = lambda a: a.reshape(-1, a.shape[-1])
+
+    ahead = passed_along(emitted[0], "section", 1)
+    rows_a = passed_along(exchanged(first_rows(emitted[0], row), S), "section", 1)
+    rows_k = passed_along(exchanged(first_rows(stash[0], row), S), "section", size // 2)
+    kept = passed_along(stash[0], "section", size // 2)
+    top = passed_along(returned[0], "section", -1)
+
+    ahead = lined(ahead)
+    for l in range(L):
+        mixed, _ = modes_forward(spec, l, rows_a, col, col_t, W)
+        made = field_forward(ahead, flat(exchanged(mixed, S)), skip[l], up[l], down[l], back, row_t, W, l < L - 1)
+        ahead = made[0]
+        if l < L - 1:
+            rows_a = exchanged(made[1], S)
+    sent = plain(ahead)
+
+    kept = lined(kept)
+    saved = []
+    for l in range(L):
+        mixed, modes = modes_forward(spec, l, rows_k, col, col_t, W)
+        arrived = flat(exchanged(mixed, S))
+        saved.append((kept, arrived, modes))
+        if l < L - 1:
+            kept, rows_k = field_forward(kept, arrived, skip[l], up[l], down[l], back, row_t, W, True)
+            rows_k = exchanged(rows_k, S)
+    g = lined(top)
+    spec_grad = None
+    skips, ups, downs = [], [], []
+    for l in reversed(range(L)):
+        v, arrived, modes = saved[l]
+        gz, rows, gs, gu, gd = field_backward(v, g, arrived, skip[l], up[l], down[l], up_t[l], down_t[l], back, back_t, W)
+        mixed, spec_grad = modes_backward(spec, l, exchanged(rows, S), modes, col, col_t, W, spec_grad)
+        g = field_grad(g, gz, flat(exchanged(mixed, S)), skip_t[l], row)
+        skips.insert(0, gs[:C, :C])
+        ups.insert(0, gu[:, :C])
+        downs.insert(0, gd[:C])
+    summed = lax.psum((jnp.stack(skips) / W, jnp.stack(ups) / W, jnp.stack(downs) / W), "slab")
+    return (sent[None], plain(g)[None], summed[0][None], summed[1][None], summed[2][None], spec_grad[None])
+
+
+def work(*args):
+    H = args[0].shape[2]
+    K = args[6].shape[2]
+    if H % 128 == 0 and K % 16 == 0 and H % HB == 0 and args[6].shape[6] == 128 and 2 * K * lax.axis_size("slab") == 128:
+        return fast_shards(*args)
+    return shards(*args)
+
+
 def solution(mesh):
     placed = (
         P("section", None, "slab", None),
@@ -231,7 +665,7 @@
         P("section", None, "slab", None, None, None, None),
     )
     return jax.shard_map(
-        shards,
+        work,
         mesh=mesh,
         in_specs=placed,
         out_specs=(

time: 786 us -> 721 us (0.917)
  Pallas kernels: 0 us -> 433 us
  local copies, waits for them, and re-layouts: 311 us -> 65.1 us
  matrix products: 231 us -> 0 us
  other arithmetic: 72.4 us -> 0.06 us
  waiting for transfers between devices: 78.2 us -> 133 us
    pallas_call x0 -> x15, Pallas kernels: none -> 433 us  [the longest x3 164 us: field_forward(): call(body, (steps,), [block, same(src.shape), same(skip.shape), same(up.s...]
    dot_general x45 -> x0, matrix products: 231 us -> none  [product(): return jnp.einsum(form, left, right, preferred_element_type=jnp.float32)]
    unnamed x193 -> x51, local copies, waits for them, and re-layouts: 171 us -> 40.5 us
    ppermute x2 -> x5, waiting for transfers between devices: 24.5 us -> 87.7 us  [passed_along(): return lax.ppermute(block, axis, route)]
    all_to_all x24 -> x0, local copies, waits for them, and re-layouts: 58.7 us -> none  [the longest x12 34.7 us: to_rows(): lax.all_to_all(back_spec, 'slab', split_axis=3, concat_axis=0, tiled=True)]
    convert_element_type x12 -> x0, local copies, waits for them, and re-layouts: 54.3 us -> none  [the longest x4 30.3 us: layer_forward(): product('kqcx,phqx->kpch', mixed_modes, col_table).astype(jnp.bfloat16)]
    ppermute x1 -> x0, waiting for transfers between devices: 36.2 us -> none  [from_partner(): lax.ppermute(array, axis, [(i, i ^ 1 << stride) for i in range(lax.axis_s...]
    all_to_all x12, waiting for transfers between devices: 17.5 us -> 45 us  [exchanged(): lax.all_to_all(blocks, 'slab', split_axis=0, concat_axis=0, tiled=True)]
  transfers between devices with their start and end apart: 15 -> 17, of which waited for: 5 -> 8; matrix products, arithmetic and copies ran while one was open for 40% -> 8% of each run, Pallas kernels for 0% -> 48%
where the time goes in v1:
time: 721 us; the launch traced here: 717 us
  Pallas kernels  433 us (60%)
  waiting for transfers between devices  133 us (18%)
  local copies, waits for them, and re-layouts  65.1 us (9%)
  starting transfers between devices  61.5 us (9%)
  blocking collectives  23.5 us (3%)
    pallas_call x3, Pallas kernels, field_forward(): call(body, (steps,), [block, same(src.shape), same(skip.shape), same(up.s...  164 us
    pallas_call x2, Pallas kernels, field_backward(): call(body, (steps,), [block, block] + [same(a.shape) for a in args[2:]],...  163 us
    ppermute x5, waiting for transfers between devices, passed_along(): return lax.ppermute(block, axis, route)  87.7 us
    all_to_all x12, starting transfers between devices, exchanged(): lax.all_to_all(blocks, 'slab', split_axis=0, concat_axis=0, tiled=True)  55.6 us
    pallas_call x4, Pallas kernels, modes_forward(): call(body, (K,), [pl.BlockSpec((1, 1, 2, C, C, X), lambda i: (layer, i, 0...  45.7 us
    all_to_all x12, waiting for transfers between devices, exchanged(): lax.all_to_all(blocks, 'slab', split_axis=0, concat_axis=0, tiled=True)  45 us
    unnamed x51, local copies, waits for them, and re-layouts  40.5 us
    pallas_call x2, Pallas kernels, modes_backward(): call(body, (K,), ins, ([same(src.shape), block], [jax.ShapeDtypeStruct(sr...  27.7 us
  transfers between devices with their start and end apart: 17, of which 8 were waited for; matrix products, arithmetic and copies ran while one was open for 8% of the time, Pallas kernels for 48%

profile of v1, /device:TPU:0, one launch (start us, length us, event | category | flops | bytes accessed | tf_op | source)
XLA Modules:
  0.0 716.6 jit_solution(13847218581273350033)
XLA Ops:
  4.9 6.3 all-to-all-start.4
  12.8 15.9 %all-to-all-done.4 = bf16[4,32,2560]{2,1,0:T(8,128)(2,1)} async-done(((bf16[4,32,2560]{2,1,0:T(8,128)(2,1)}), bf16[4,32,2560]{2,1,0:T(8,128)(2,1)}, u32[]{:S(2)}, u32[]{:S(2)}) %all-to-all-start.4) | async-done | bytes 655392 | tf_op jit(solution)/shard_map/all_to_all | solution.py:588
  30.2 7.9 %copy.84 = bf16[1,2,16,2,20,20,128]{6,5,4,3,2,1,0:T(8,128)(2,1)} copy(bf16[1,2,16,2,20,20,128]{6,3,5,4,2,1,0:T(2,128)(2,1)} %param.19) | data formatting | bytes 13107200 | tf_op args[6]
  38.1 45.7 %collective-permute-done.4.src_ref = bf16[4,32,2560]{2,1,0:T(8,128)(2,1)S(1)} collective-permute-done((bf16[4,32,2560]{2,1,0:T(8,128)(2,1)}, bf16[4,32,2560]{2,1,0:T(8,128)(2,1)S(1)}, u32[]{:S(2)}, u32[]{:S(2)}) %collective-permute-start.4) | collective-permute-done | bytes 655392 | tf_op jit(solution)/shard_map/ppermute | solution.py:24
  84.7 11.4 %shard_map.178 = (bf16[4,32,2560]{2,1,0:T(8,128)(2,1)}, bf16[320,256]{1,0:T(8,128)(2,1)}) custom-call(bf16[2,16,2,20,20,128]{5,4,3,2,1,0:T(8,128)(2,1)} %bitcast.89, bf16[4,32,2560]{2,1,0:T(8,128)(2,1)} %copy-done.8, bf16[1024,256]{1,0:T(8,128)(2,1)} %constant.26.clone.col_ref, bf16[256,1024]{1,0:T(8,128)(2,1)} %constant.27.clone.colt_ref), custom_call_target="tpu_custom_call" | custom-call | flops 335544320 | bytes 6553600 | tf_op jit(solution)/shard_map/pallas_call | solution.py:351
  107.4 9.4 %all-to-all-done.5 = bf16[4,32,2560]{2,1,0:T(8,128)(2,1)S(1)} async-done(((bf16[4,32,2560]{2,1,0:T(8,128)(2,1)}), bf16[4,32,2560]{2,1,0:T(8,128)(2,1)S(1)}, u32[]{:S(2)}, u32[]{:S(2)}) %all-to-all-start.5) | async-done | bytes 655392 | tf_op jit(solution)/shard_map/all_to_all | solution.py:588
  117.6 55.7 %shard_map.179 = (bf16[128,32,512]{2,1,0:T(8,128)(2,1)}, bf16[128,2560]{1,0:T(8,128)(2,1)}) custom-call(bf16[128,32,512]{2,1,0:T(8,128)(2,1)} %pad.27.v_ref, bf16[128,2560]{1,0:T(8,128)(2,1)} %bitcast.108, bf16[32,32]{1,0:T(8,128)(2,1)} %copy.55.skip_ref, bf16[80,32]{1,0:T(8,128)(2,1)} %copy.56.up_ref, bf16[32,80]{1,0:T(8,128)(2,1)} %copy.57.down_ref, ...), custom_call_target="tpu_custom_call" | custom-call | flops 1744830464 | bytes 8388608 | tf_op jit(solution)/shard_map/pallas_call | solution.py:488
  181.1 12.5 %all-to-all-done.6.src_ref = bf16[4,32,2560]{2,1,0:T(8,128)(2,1)S(1)} async-done(((bf16[4,32,2560]{2,1,0:T(8,128)(2,1)}), bf16[4,32,2560]{2,1,0:T(8,128)(2,1)S(1)}, u32[]{:S(2)}, u32[]{:S(2)}) %all-to-all-start.6) | async-done | bytes 655392 | tf_op jit(solution)/shard_map/all_to_all | solution.py:588
  198.3 11.5 %shard_map.180 = (bf16[4,32,2560]{2,1,0:T(8,128)(2,1)}, bf16[320,256]{1,0:T(8,128)(2,1)}) custom-call(bf16[2,16,2,20,20,128]{5,4,3,2,1,0:T(8,128)(2,1)} %bitcast.90, bf16[4,32,2560]{2,1,0:T(8,128)(2,1)} %copy-done.6, bf16[1024,256]{1,0:T(8,128)(2,1)} %constant.26.clone.col_ref, bf16[256,1024]{1,0:T(8,128)(2,1)} %constant.27.clone.colt_ref), custom_call_target="tpu_custom_call" | custom-call | flops 335544320 | bytes 6553600 | tf_op jit(solution)/shard_map/pallas_call | solution.py:351
  222.6 41.9 %collective-permute-done.1.src_ref = bf16[4,32,2560]{2,1,0:T(8,128)(2,1)S(1)} collective-permute-done((bf16[4,32,2560]{2,1,0:T(8,128)(2,1)}, bf16[4,32,2560]{2,1,0:T(8,128)(2,1)S(1)}, u32[]{:S(2)}, u32[]{:S(2)}) %collective-permute-start.1) | collective-permute-done | bytes 655392 | tf_op jit(solution)/shard_map/ppermute | solution.py:24
  265.4 11.4 %shard_map.173 = (bf16[4,32,2560]{2,1,0:T(8,128)(2,1)}, bf16[320,256]{1,0:T(8,128)(2,1)}) custom-call(bf16[2,16,2,20,20,128]{5,4,3,2,1,0:T(8,128)(2,1)} %bitcast.91, bf16[4,32,2560]{2,1,0:T(8,128)(2,1)} %copy-done.7, bf16[1024,256]{1,0:T(8,128)(2,1)} %constant.26.clone.col_ref, bf16[256,1024]{1,0:T(8,128)(2,1)} %constant.27.clone.colt_ref), custom_call_target="tpu_custom_call" | custom-call | flops 335544320 | bytes 6553600 | tf_op jit(solution)/shard_map/pallas_call | solution.py:351
  288.9 81.3 %shard_map.181 = (bf16[128,32,512]{2,1,0:T(8,128)(2,1)}, bf16[128,2560]{1,0:T(8,128)(2,1)}, f32[32,32]{1,0:T(8,128)}, f32[80,32]{1,0:T(8,128)}, f32[32,80]{1,0:T(8,128)}) custom-call(bf16[128,32,512]{2,1,0:T(8,128)(2,1)} %get-tuple-element.35.v_ref, bf16[128,32,512]{2,1,0:T(8,128)(2,1)} %pad.26.g_ref, bf16[128,2560]{1,0:T(8,128)(2,1)} %bitcast.25.src_ref, ...), custom_call_target="tpu_custom_call" | custom-call | flops 3489660928 | bytes 12582912 | tf_op jit(solution)/shard_map/pallas_call | solution.py:542
  380.3 55.7 %shard_map.174 = (bf16[128,32,512]{2,1,0:T(8,128)(2,1)}, bf16[128,2560]{1,0:T(8,128)(2,1)}) custom-call(bf16[128,32,512]{2,1,0:T(8,128)(2,1)} %pad.22.v_ref, bf16[128,2560]{1,0:T(8,128)(2,1)} %bitcast.110, bf16[32,32]{1,0:T(8,128)(2,1)} %copy.55.skip_ref, bf16[80,32]{1,0:T(8,128)(2,1)} %copy.56.up_ref, bf16[32,80]{1,0:T(8,128)(2,1)} %copy.57.down_ref, ...), custom_call_target="tpu_custom_call" | custom-call | flops 1744830464 | bytes 8388608 | tf_op jit(solution)/shard_map/pallas_call | solution.py:488
  436.0 5.1 all-to-all-start.2
  441.1 13.9 %shard_map.182 = (bf16[4,32,2560]{2,1,0:T(8,128)(2,1)}, f32[2,16,2,20,20,128]{5,4,3,2,1,0:T(8,128)}) custom-call(bf16[2,16,2,20,20,128]{5,4,3,2,1,0:T(8,128)(2,1)} %bitcast.92, bf16[4,32,2560]{2,1,0:T(8,128)(2,1)} %copy-done.4, bf16[320,256]{1,0:T(8,128)(2,1)} %get-tuple-element.40.m_ref, bf16[1024,256]{1,0:T(8,128)(2,1)} %constant.26.clone.col_ref, ...), custom_call_target="tpu_custom_call" | custom-call | flops 335544320 | bytes 13107200 | tf_op jit(solution)/shard_map/pallas_call | solution.py:401
  460.1 11.4 %shard_map.175 = (bf16[4,32,2560]{2,1,0:T(8,128)(2,1)}, bf16[320,256]{1,0:T(8,128)(2,1)}) custom-call(bf16[2,16,2,20,20,128]{5,4,3,2,1,0:T(8,128)(2,1)} %bitcast.93, bf16[4,32,2560]{2,1,0:T(8,128)(2,1)} %copy-done.5, bf16[1024,256]{1,0:T(8,128)(2,1)} %constant.26.clone.col_ref, bf16[256,1024]{1,0:T(8,128)(2,1)} %constant.27.clone.colt_ref), custom_call_target="tpu_custom_call" | custom-call | flops 335544320 | bytes 6553600 | tf_op jit(solution)/shard_map/pallas_call | solution.py:351
  478.5 12.3 %shard_map.183.g_ref = bf16[128,32,512]{2,1,0:T(8,128)(2,1)} custom-call(bf16[128,32,512]{2,1,0:T(8,128)(2,1)} %pad.26.g_ref, bf16[128,32,512]{2,1,0:T(8,128)(2,1)} %get-tuple-element.38.gz_ref, bf16[128,2560]{1,0:T(8,128)(2,1)} %bitcast.101, bf16[32,32]{1,0:T(8,128)(2,1)} %get-tuple-element.74.skipt_ref, bf16[128,512]{1,0:T(8,128)(2,1)} %constant.22.clone.row_ref), custom_call_target="tpu_custom_call" | custom-call | flops 536870912 | bytes 12582912 | tf_op jit(solution)/shard_map/pallas_call | solution.py:577
  490.8 81.3 %shard_map.184 = (bf16[128,32,512]{2,1,0:T(8,128)(2,1)}, bf16[128,2560]{1,0:T(8,128)(2,1)}, f32[32,32]{1,0:T(8,128)}, f32[80,32]{1,0:T(8,128)}, f32[32,80]{1,0:T(8,128)}) custom-call(bf16[128,32,512]{2,1,0:T(8,128)(2,1)} %pad.27.v_ref, bf16[128,32,512]{2,1,0:T(8,128)(2,1)} %shard_map.183.g_ref, bf16[128,2560]{1,0:T(8,128)(2,1)} %bitcast.109, ...), custom_call_target="tpu_custom_call" | custom-call | flops 3489660928 | bytes 12582912 | tf_op jit(solution)/shard_map/pallas_call | solution.py:542
  576.9 52.3 %shard_map.176 = bf16[128,32,512]{2,1,0:T(8,128)(2,1)} custom-call(bf16[128,32,512]{2,1,0:T(8,128)(2,1)} %get-tuple-element.31.v_ref, bf16[128,2560]{1,0:T(8,128)(2,1)} %bitcast.99, bf16[32,32]{1,0:T(8,128)(2,1)} %copy.58.skip_ref, bf16[80,32]{1,0:T(8,128)(2,1)} %copy.59.up_ref, bf16[32,80]{1,0:T(8,128)(2,1)} %copy.60.down_ref, ...), custom_call_target="tpu_custom_call" | custom-call | flops 1744830464 | bytes 8388608 | tf_op jit(solution)/shard_map/pallas_call | solution.py:488
  634.6 13.8 %shard_map.185 = (bf16[4,32,2560]{2,1,0:T(8,128)(2,1)}, f32[2,16,2,20,20,128]{5,4,3,2,1,0:T(8,128)}) custom-call(bf16[2,16,2,20,20,128]{5,4,3,2,1,0:T(8,128)(2,1)} %bitcast.94, bf16[4,32,2560]{2,1,0:T(8,128)(2,1)} %copy-done.2, bf16[320,256]{1,0:T(8,128)(2,1)} %get-tuple-element.44.m_ref, ...), custom_call_target="tpu_custom_call", output_to_operand_aliasing={{1}: (5, {})} | custom-call | flops 335544320 | bytes 13107200 | tf_op jit(solution)/shard_map/pallas_call | solution.py:401
  648.4 5.1 all-to-all-start.11
  653.7 23.5 %all-reduce.6 = (f32[1,2,20,20]{3,2,1,0:T(8,128)S(1)}, f32[1,2,80,20]{2,1,3,0:T(2,128)}, f32[1,2,20,80]{3,2,1,0:T(8,128)S(1)}) all-reduce(f32[1,2,20,20]{3,2,1,0:T(8,128)S(1)} %fusion, f32[1,2,80,20]{2,1,3,0:T(2,128)S(1)} %fusion.4, f32[1,2,20,80]{3,2,1,0:T(8,128)S(1)} %fusion.1), channel_id=1, replica_groups=mesh['section'=8,'slab'=4] {'slab'}, use_global_device_ids=true, to_apply=%region_0.1 | all-reduce | flops 7200 | bytes 57600 | tf_op jit(solution)/shard_map/psum | solution.py:645
  678.5 20.4 %copy.78 = f32[1,2,16,2,20,20,128]{6,3,5,4,2,1,0:T(2,128)} copy(f32[1,2,16,2,20,20,128]{6,5,4,3,2,1,0:T(8,128)} %bitcast.95) | data formatting | bytes 26214400
  699.8 12.3 %shard_map.186 = bf16[128,32,512]{2,1,0:T(8,128)(2,1)} custom-call(bf16[128,32,512]{2,1,0:T(8,128)(2,1)} %shard_map.183.g_ref, bf16[128,32,512]{2,1,0:T(8,128)(2,1)} %get-tuple-element.42.gz_ref, bf16[128,2560]{1,0:T(8,128)(2,1)} %bitcast.100, bf16[32,32]{1,0:T(8,128)(2,1)} %get-tuple-element.73.skipt_ref, bf16[128,512]{1,0:T(8,128)(2,1)} %constant.22.clone.row_ref), custom_call_target="tpu_custom_call" | custom-call | flops 536870912 | bytes 12582912 | tf_op jit(solution)/shard_map/pallas_call | solution.py:577
  (111 shorter events, 97.7 us)
Async XLA Ops:
  4.9 23.7 %all-to-all-start.4 = ((bf16[4,32,2560]{2,1,0:T(8,128)(2,1)}), bf16[4,32,2560]{2,1,0:T(8,128)(2,1)}, u32[]{:S(2)}, u32[]{:S(2)}) async-start(bf16[4,32,2560]{2,1,0:T(8,128)(2,1)} %bitcast.107), calls=%async_computation.4 | async-start | bytes 1310720 | tf_op jit(solution)/shard_map/all_to_all | solution.py:588
  11.3 92.0 %collective-permute-start.3 = (bf16[20,128,512]{2,1,0:T(8,128)(2,1)}, bf16[20,128,512]{2,1,0:T(8,128)(2,1)S(1)}, u32[]{:S(2)}, u32[]{:S(2)}) collective-permute-start(bf16[20,128,512]{2,1,0:T(8,128)(2,1)} %bitcast.103), channel_id=1, source_target_pairs={{16,0},{20,4},{24,8},{28,12},{0,16},{4,20},{8,24},{12,28},{17,1},{... | collective-permute-start | bytes 7864328 | tf_op jit(solution)/shard_map/ppermute | solution.py:24
  28.7 55.2 %collective-permute-start.4 = (bf16[4,32,2560]{2,1,0:T(8,128)(2,1)}, bf16[4,32,2560]{2,1,0:T(8,128)(2,1)S(1)}, u32[]{:S(2)}, u32[]{:S(2)}) collective-permute-start(bf16[4,32,2560]{2,1,0:T(8,128)(2,1)} %all-to-all-done.4), channel_id=1, source_target_pairs={{16,0},{20,4},{24,8},{28,12},{0,16},{4,20},{8,24},{12,28},{17,1},{... | collective-permute-start | bytes 1966088 | tf_op jit(solution)/shard_map/ppermute | solution.py:24
  84.7 16.2 %copy-start.16 = (bf16[1,2,20,80]{3,1,2,0:T(2,128)(2,1)S(1)}, bf16[1,2,20,80]{3,1,2,0:T(2,128)(2,1)}, u32[]{:S(2)}) copy-start(bf16[1,2,20,80]{3,1,2,0:T(2,128)(2,1)} %param.18) | copy-start | bytes 19204
  84.7 17.0 %copy-start.14 = (bf16[1,2,80,20]{2,1,3,0:T(2,128)(2,1)S(1)}, bf16[1,2,80,20]{2,1,3,0:T(2,128)(2,1)}, u32[]{:S(2)}) copy-start(bf16[1,2,80,20]{2,1,3,0:T(2,128)(2,1)} %param.17) | copy-start | bytes 19204
  84.7 17.8 %copy-start.15 = (bf16[1,2,20,20]{3,1,2,0:T(2,128)(2,1)S(1)}, bf16[1,2,20,20]{3,1,2,0:T(2,128)(2,1)}, u32[]{:S(2)}) copy-start(bf16[1,2,20,20]{3,1,2,0:T(2,128)(2,1)} %param.16) | copy-start | bytes 4804
  96.1 20.7 %all-to-all-start.5 = ((bf16[4,32,2560]{2,1,0:T(8,128)(2,1)}), bf16[4,32,2560]{2,1,0:T(8,128)(2,1)S(1)}, u32[]{:S(2)}, u32[]{:S(2)}) async-start(bf16[4,32,2560]{2,1,0:T(8,128)(2,1)} %get-tuple-element.34), calls=%async_computation.5 | async-start | bytes 1310720 | tf_op jit(solution)/shard_map/all_to_all | solution.py:588
  173.3 20.2 %all-to-all-start.6 = ((bf16[4,32,2560]{2,1,0:T(8,128)(2,1)}), bf16[4,32,2560]{2,1,0:T(8,128)(2,1)S(1)}, u32[]{:S(2)}, u32[]{:S(2)}) async-start(bf16[4,32,2560]{2,1,0:T(8,128)(2,1)} %bitcast.114), calls=%async_computation.6 | async-start | bytes 1310720 | tf_op jit(solution)/shard_map/all_to_all | solution.py:588
  193.5 20.3 %all-to-all-start = ((bf16[4,32,2560]{2,1,0:T(8,128)(2,1)}), bf16[4,32,2560]{2,1,0:T(8,128)(2,1)S(1)}, u32[]{:S(2)}, u32[]{:S(2)}) async-start(bf16[4,32,2560]{2,1,0:T(8,128)(2,1)} %bitcast.106), calls=%async_computation | async-start | bytes 1310720 | tf_op jit(solution)/shard_map/all_to_all | solution.py:588
  197.0 86.0 %collective-permute-start.2 = (bf16[20,128,512]{2,1,0:T(8,128)(2,1)}, bf16[20,128,512]{2,1,0:T(8,128)(2,1)}, u32[]{:S(2)}, u32[]{:S(2)}) collective-permute-start(bf16[20,128,512]{2,1,0:T(8,128)(2,1)} %bitcast.121), channel_id=1, source_target_pairs={{4,0},{8,4},{12,8},{16,12},{20,16},{24,20},{28,24},{0,28},{5,1},{9... | collective-permute-start | bytes 7864328 | tf_op jit(solution)/shard_map/ppermute | solution.py:24
  214.7 62.1 %all-to-all-start.7 = ((bf16[4,32,2560]{2,1,0:T(8,128)(2,1)}), bf16[4,32,2560]{2,1,0:T(8,128)(2,1)}, u32[]{:S(2)}, u32[]{:S(2)}) async-start(bf16[4,32,2560]{2,1,0:T(8,128)(2,1)} %get-tuple-element.37), calls=%async_computation.7 | async-start | bytes 1310720 | tf_op jit(solution)/shard_map/all_to_all | solution.py:588
  218.9 157.2 %collective-permute-start = (bf16[20,128,512]{2,1,0:T(8,128)(2,1)}, bf16[20,128,512]{2,1,0:T(8,128)(2,1)S(1)}, u32[]{:S(2)}, u32[]{:S(2)}) collective-permute-start(bf16[20,128,512]{2,1,0:T(8,128)(2,1)} %bitcast.105), channel_id=1, source_target_pairs={{28,0},{0,4},{4,8},{8,12},{12,16},{16,20},{20,24},{24,28},{29,1},{... | collective-permute-start | bytes 7864328 | tf_op jit(solution)/shard_map/ppermute | solution.py:24
  218.9 45.6 %collective-permute-start.1 = (bf16[4,32,2560]{2,1,0:T(8,128)(2,1)}, bf16[4,32,2560]{2,1,0:T(8,128)(2,1)S(1)}, u32[]{:S(2)}, u32[]{:S(2)}) collective-permute-start(bf16[4,32,2560]{2,1,0:T(8,128)(2,1)} %copy-done.11), channel_id=1, source_target_pairs={{28,0},{0,4},{4,8},{8,12},{12,16},{16,20},{20,24},{24,28},{29,1},{... | collective-permute-start | bytes 1966088 | tf_op jit(solution)/shard_map/ppermute | solution.py:24
  276.8 93.4 %all-to-all-start.1 = ((bf16[4,32,2560]{2,1,0:T(8,128)(2,1)}), bf16[4,32,2560]{2,1,0:T(8,128)(2,1)S(1)}, u32[]{:S(2)}, u32[]{:S(2)}) async-start(bf16[4,32,2560]{2,1,0:T(8,128)(2,1)} %get-tuple-element.30), calls=%async_computation.1 | async-start | bytes 1310720 | tf_op jit(solution)/shard_map/all_to_all | solution.py:588
  371.0 65.0 %all-to-all-start.8 = ((bf16[4,32,2560]{2,1,0:T(8,128)(2,1)}), bf16[4,32,2560]{2,1,0:T(8,128)(2,1)S(1)}, u32[]{:S(2)}, u32[]{:S(2)}) async-start(bf16[4,32,2560]{2,1,0:T(8,128)(2,1)} %bitcast.112), calls=%async_computation.8 | async-start | bytes 1310720 | tf_op jit(solution)/shard_map/all_to_all | solution.py:588
  436.0 19.6 %all-to-all-start.2 = ((bf16[4,32,2560]{2,1,0:T(8,128)(2,1)}), bf16[4,32,2560]{2,1,0:T(8,128)(2,1)S(1)}, u32[]{:S(2)}, u32[]{:S(2)}) async-start(bf16[4,32,2560]{2,1,0:T(8,128)(2,1)} %bitcast.113), calls=%async_computation.2 | async-start | bytes 1310720 | tf_op jit(solution)/shard_map/all_to_all | solution.py:588
  455.6 18.4 %all-to-all-start.9 = ((bf16[4,32,2560]{2,1,0:T(8,128)(2,1)}), bf16[4,32,2560]{2,1,0:T(8,128)(2,1)S(1)}, u32[]{:S(2)}, u32[]{:S(2)}) async-start(bf16[4,32,2560]{2,1,0:T(8,128)(2,1)} %get-tuple-element.41), calls=%async_computation.9 | async-start | bytes 1310720 | tf_op jit(solution)/shard_map/all_to_all | solution.py:588
  460.1 18.3 %copy-start.12 = (f32[80,32]{1,0:T(8,128)S(1)}, f32[80,32]{1,0:T(8,128)}, u32[]{:S(2)}) copy-start(f32[80,32]{1,0:T(8,128)} %get-tuple-element.50) | copy-start | bytes 30724
  474.0 98.0 %all-to-all-start.3 = ((bf16[4,32,2560]{2,1,0:T(8,128)(2,1)}), bf16[4,32,2560]{2,1,0:T(8,128)(2,1)S(1)}, u32[]{:S(2)}, u32[]{:S(2)}) async-start(bf16[4,32,2560]{2,1,0:T(8,128)(2,1)} %get-tuple-element.33), calls=%async_computation.3 | async-start | bytes 1310720 | tf_op jit(solution)/shard_map/all_to_all | solution.py:588
  572.1 61.7 %all-to-all-start.10 = ((bf16[4,32,2560]{2,1,0:T(8,128)(2,1)}), bf16[4,32,2560]{2,1,0:T(8,128)(2,1)S(1)}, u32[]{:S(2)}, u32[]{:S(2)}) async-start(bf16[4,32,2560]{2,1,0:T(8,128)(2,1)} %bitcast.111), calls=%async_computation.10 | async-start | bytes 1310720 | tf_op jit(solution)/shard_map/all_to_all | solution.py:588
  634.6 18.9 %copy-start.13 = (f32[80,32]{1,0:T(8,128)S(1)}, f32[80,32]{1,0:T(8,128)}, u32[]{:S(2)}) copy-start(f32[80,32]{1,0:T(8,128)} %get-tuple-element.49) | copy-start | bytes 30724
  634.6 19.1 %copy-start.20 = (f32[32,80]{1,0:T(8,128)S(1)}, f32[32,80]{1,0:T(8,128)}, u32[]{:S(2)}) copy-start(f32[32,80]{1,0:T(8,128)} %get-tuple-element.51) | copy-start | bytes 30724
  634.6 19.1 %copy-start.19 = (f32[32,32]{1,0:T(8,128)S(1)}, f32[32,32]{1,0:T(8,128)}, u32[]{:S(2)}) copy-start(f32[32,32]{1,0:T(8,128)} %get-tuple-element.47) | copy-start | bytes 12292
  648.4 50.5 %all-to-all-start.11 = ((bf16[4,32,2560]{2,1,0:T(8,128)(2,1)}), bf16[4,32,2560]{2,1,0:T(8,128)(2,1)S(1)}, u32[]{:S(2)}, u32[]{:S(2)}) async-start(bf16[4,32,2560]{2,1,0:T(8,128)(2,1)} %get-tuple-element.46), calls=%async_computation.11 | async-start | bytes 1310720 | tf_op jit(solution)/shard_map/all_to_all | solution.py:588
  (14 other events, 34.3 us)
